TPU v7x, 32 devices: a whole 2x2x4 slice. The times are simulated.
32 devices in a mesh: blk: 16 (over z, y, x), phe: 2 (over core).
Axes of the slice: x: 2, y: 2, z: 4, core: 2. Of those that a mesh axis runs over, the one named last changes fastest.
Arguments:
- ld_rows: bfloat16 [16384, 1024], P('blk'), may hold values from -1.5 to 1.5, as said below
- block_first: int32 [16384], P('blk'), may hold values from 0 to 16383, as said below
- beta_hat: float32 [128, 16384], P('phe', 'blk'), may hold values from -6 to 6
- psi: float32 [128, 16384], P('phe', 'blk'), may hold values from 0.05 to 5
- noise: bfloat16 [3, 128, 16384], P(None, 'phe', 'blk'), may hold values from -5 to 5
- sample_size: int32 [128], P('phe'), may hold values from 2000 to 199999
Outputs:
- effects: float32 [128, 16384], P('phe', 'blk')
Inputs may be any that keep to these rules, and one draw needn't show every extreme that they name: block_first[j] is the first SNP of the run of consecutive SNPs that forms j's LD block; every block holds 128 to 1024 SNPs, except the last block, which ends at SNP 16384 - 1 and may hold fewer. ld_rows[j, c] is the LD between SNP j and SNP block_first[j] + c for c below the length of j's block, and zero for larger c; every block's matrix is symmetric with unit diagonal.
All inputs are finite; a program needn't handle non-finite values.
Results may differ from a plain program's by a relative error of at most 0.00055.
The roundings to bfloat16 on the way count: a program that leaves them out, or rounds other values in their place, can miss the bound.
Values may be sent and summed in bfloat16 or wider, within the bound.
No kernel may reach another device: no remote copies, remote signals or barrier semaphores. Data moves between devices by JAX's collectives and lax.ppermute only.
A program may use at most 64 MiB of HBM per device.

v0:
```python
import jax
import jax.numpy as jnp
from jax import lax
from jax.sharding import PartitionSpec as P

ITERS = 3
SLOTS = 10
tiny_term = 1e-06
sample_ref = 20000.0


def extended_2(cells, sides, width):
    for axis, dim in sides:
        count = lax.axis_size(axis)
        ends = count - 1
        head = lax.slice_in_dim(cells, 0, width, axis=dim)
        tail = lax.slice_in_dim(cells, cells.shape[dim] - width, cells.shape[dim], axis=dim)
        cells = jnp.concatenate(
            [
                lax.ppermute(tail, axis, [(i, (i + 1) % count) for i in range(ends)]),
                cells,
                lax.ppermute(head, axis, [((i + 1) % count, i) for i in range(ends)]),
            ],
            axis=dim,
        )
    return cells


def shards(ld_rows, block_first, beta_hat, psi, noise, sample_size):
    snp_local = ld_rows.shape[0]
    span = ld_rows.shape[1]
    pheno_local = beta_hat.shape[0]
    total_snps = snp_local * lax.axis_size("blk")
    total_pheno = pheno_local * lax.axis_size("phe")
    base_row = lax.axis_index("blk") * snp_local
    positions = jnp.arange(snp_local, dtype=jnp.int32)
    start_mask = (block_first == base_row + positions) | (positions == 0)
    seg_first = jnp.nonzero(start_mask, size=SLOTS, fill_value=snp_local)[0].astype(jnp.int32)
    seg_count = jnp.sum(start_mask.astype(jnp.int32))
    seg_next = jnp.concatenate([seg_first[1:], jnp.full((1,), snp_local, jnp.int32)])
    seg_rows = seg_next - seg_first
    clipped = jnp.minimum(seg_first, snp_local - 1)
    seg_col = block_first[clipped] - base_row + span
    ld_padded = jnp.pad(ld_rows, ((0, span), (0, 0)))
    offsets = jnp.arange(span, dtype=jnp.int32)
    beta = jnp.zeros(beta_hat.shape, jnp.float32)
    for iteration in range(ITERS):
        rounded = beta.astype(jnp.bfloat16)
        weighted = beta * beta / psi
        scale_local = jnp.sum(weighted, axis=1)
        scale_total = lax.psum(scale_local, "blk")
        extended = extended_2(rounded, (("blk", 1),), span)

        def one_piece(number, result):
            row_start = seg_first[number]
            ld_tile = lax.dynamic_slice_in_dim(ld_padded, row_start, span, 0)
            window = lax.dynamic_slice_in_dim(extended, seg_col[number], span, 1)
            product = lax.dot_general(
                window, ld_tile, (((1,), (1,)), ((), ())), preferred_element_type=jnp.float32
            )
            product = jnp.where((offsets < seg_rows[number])[None, :], product, jnp.float32(0.0))
            current = lax.dynamic_slice_in_dim(result, row_start, span, 1)
            return lax.dynamic_update_slice_in_dim(result, current + product, row_start, 1)

        start_value = jnp.zeros((pheno_local, snp_local + span), jnp.float32)
        result = lax.fori_loop(0, seg_count, one_piece, start_value)
        applied = result[:, :snp_local]
        grad = beta_hat - applied
        resid_local = jnp.sum(grad * grad, axis=1)
        resid_total = lax.psum(resid_local, "blk")
        pooled_total = lax.psum(jnp.sum(scale_total), "phe")
        pooled = pooled_total / (total_snps * total_pheno) + tiny_term
        scale = scale_total / total_snps + tiny_term
        resid = resid_total / total_snps + tiny_term
        phi = (scale + pooled) / 2.0
        amp = jnp.sqrt(resid * sample_ref / sample_size.astype(jnp.float32))
        shrink = psi / (psi + phi[:, None])
        beta = shrink * (beta + grad + amp[:, None] * noise[iteration].astype(jnp.float32))
    return beta


def solution(mesh):
    in_specs = (
        P("blk", None),
        P("blk"),
        P("phe", "blk"),
        P("phe", "blk"),
        P(None, "phe", "blk"),
        P("phe"),
    )
    out_specs = P("phe", "blk")
    return jax.shard_map(shards, mesh=mesh, in_specs=in_specs, out_specs=out_specs, check_vma=False)
```

profile of v0, /device:TPU:0, one launch (start us, length us, event | category | flops | bytes accessed | tf_op | source)
XLA Modules:
  0.0 288.1 jit_solution(13211630202490944520)
XLA Ops:
  0.0 5.0 %collective-permute-start = (bf16[64,1024]{1,0:T(8,128)(2,1)S(1)}, bf16[64,1024]{1,0:T(8,128)(2,1)S(1)}, u32[]{:S(2)}, u32[]{:S(2)}) collective-permute-start(bf16[64,1024]{1,0:T(8,128)(2,1)S(1)} %convert_element_type.41), channel_id=1, source_target_pairs={{0,2},{2,4},{4,6},{6,8},{8,10},{10,12},{12,14},{14,16},{16,18},{18... | collective-permute-start | bytes 393224 | tf_op jit(solution)/shard_map/ppermute | solution.py:20
  7.6 7.6 %scatter_custom_fusion = s32[10]{0:T(128)S(1)} fusion(s32[1024]{0:T(1024)S(1)} %bitcast.48, s32[1024]{0:T(1024)S(1)} %broadcast.175, s32[]{:T(128)} %constant.110.clone.1), kind=kCustom, calls=%fused_computation.84 | custom fusion | flops 1024 | bytes 44 | tf_op jit(solution)/shard_map/scatter-add | solution.py:38
  18.8 4.0 %pad.4 = bf16[2048,1024]{1,0:T(8,128)(2,1)} pad(bf16[1024,1024]{1,0:T(8,128)(2,1)} %param.12, bf16[]{:T(256)} %constant.117.clone.1), padding=0_1024x0_0 | pad | bytes 6291458 | tf_op jit(solution)/shard_map/jit(_pad)/pad | solution.py:44
  23.1 30.7 %while.33 = (s32[]{:T(128)}, f32[64,2048]{1,0:T(8,128)S(1)}, s32[]{:T(128)}, s32[10]{0:T(128)S(1)}, s32[10]{0:T(128)S(1)}, /*index=5*/s32[10]{0:T(128)S(1)}, bf1...) while((s32[]{:T(128)}, f32[64,2048]{1,0:T(8,128)S(1)}, ...), condition=%wide.region_10.11_spmd.clone, body=%wide.region_9.10_spmd.clone.sunk | while | flops 134349840 | bytes 3280655 | solution.py:66
  30.0 2.4 fusion.67
  39.5 2.4 fusion.67
  50.0 2.4 fusion.67
  53.9 49.3 %all-reduce.3 = (f32[64]{0:T(128)S(1)}, f32[64]{0:T(128)S(1)}) all-reduce(f32[64]{0:T(128)S(1)} %multiply_reduce_fusion.2, f32[64]{0:T(128)S(1)} %divide_reduce_fusion), channel_id=1, replica_groups=mesh['blk'=16,'phe'=2] {'blk'}, use_global_device_ids=true, to_apply=%region_12.13 | all-reduce | flops 128 | bytes 1024 | tf_op jit(solution)/shard_map/psum | solution.py:70
  103.8 3.1 %psum.64 = f32[]{:T(128)} all-reduce(f32[]{:T(128)} %reduce_sum.95), channel_id=1, replica_groups=mesh['blk'=16,'phe'=2] {'phe'}, use_global_device_ids=true, to_apply=%region_3.4 | all-reduce | flops 1 | bytes 8 | tf_op jit(solution)/shard_map/psum | solution.py:71
  107.9 3.9 %collective-permute-start.2 = (bf16[64,1024]{1,0:T(8,128)(2,1)S(1)}, bf16[64,1024]{1,0:T(8,128)(2,1)S(1)}, u32[]{:S(2)}, u32[]{:S(2)}) collective-permute-start(bf16[64,1024]{1,0:T(8,128)(2,1)S(1)} %convert_element_type.45), channel_id=1, source_target_pairs={{0,2},{2,4},{4,6},{6,8},{8,10},{10,12},{12,14},{14,16},{16,18},{18... | collective-permute-start | bytes 393224 | tf_op jit(solution)/shard_map/ppermute | solution.py:20
  113.1 4.6 %collective-permute-done.2 = bf16[64,1024]{1,0:T(8,128)(2,1)S(1)} collective-permute-done((bf16[64,1024]{1,0:T(8,128)(2,1)S(1)}, bf16[64,1024]{1,0:T(8,128)(2,1)S(1)}, u32[]{:S(2)}, u32[]{:S(2)}) %collective-permute-start.2) | collective-permute-done | bytes 131104 | tf_op jit(solution)/shard_map/ppermute | solution.py:20
  119.1 30.6 %while.34 = (s32[]{:T(128)}, f32[64,2048]{1,0:T(8,128)S(1)}, s32[]{:T(128)}, s32[10]{0:T(128)S(1)}, s32[10]{0:T(128)S(1)}, /*index=5*/s32[10]{0:T(128)S(1)}, bf1...) while((s32[]{:T(128)}, f32[64,2048]{1,0:T(8,128)S(1)}, ...), condition=%wide.region_18.19_spmd.clone, body=%wide.region_17.18_spmd.clone.sunk | while | flops 134349840 | bytes 3280655 | solution.py:66
  125.9 2.4 fusion.70
  135.4 2.4 fusion.70
  145.9 2.4 fusion.70
  149.8 43.2 %all-reduce.2 = (f32[64]{0:T(128)S(1)}, f32[64]{0:T(128)S(1)}) all-reduce(f32[64]{0:T(128)S(1)} %multiply_reduce_fusion.1, f32[64]{0:T(128)S(1)} %get-tuple-element.265), channel_id=1, replica_groups=mesh['blk'=16,'phe'=2] {'blk'}, use_global_device_ids=true, to_apply=%region_20.21 | all-reduce | flops 128 | bytes 1024 | tf_op jit(solution)/shard_map/psum | solution.py:70
  193.7 3.1 %psum.67 = f32[]{:T(128)} all-reduce(f32[]{:T(128)} %reduce_sum.99), channel_id=1, replica_groups=mesh['blk'=16,'phe'=2] {'phe'}, use_global_device_ids=true, to_apply=%region_16.17 | all-reduce | flops 1 | bytes 8 | tf_op jit(solution)/shard_map/psum | solution.py:71
  197.7 3.9 %collective-permute-start.4 = (bf16[64,1024]{1,0:T(8,128)(2,1)S(1)}, bf16[64,1024]{1,0:T(8,128)(2,1)S(1)}, u32[]{:S(2)}, u32[]{:S(2)}) collective-permute-start(bf16[64,1024]{1,0:T(8,128)(2,1)S(1)} %convert_element_type.48), channel_id=1, source_target_pairs={{0,2},{2,4},{4,6},{6,8},{8,10},{10,12},{12,14},{14,16},{16,18},{18... | collective-permute-start | bytes 393224 | tf_op jit(solution)/shard_map/ppermute | solution.py:20
  202.9 4.6 %collective-permute-done.4 = bf16[64,1024]{1,0:T(8,128)(2,1)S(1)} collective-permute-done((bf16[64,1024]{1,0:T(8,128)(2,1)S(1)}, bf16[64,1024]{1,0:T(8,128)(2,1)S(1)}, u32[]{:S(2)}, u32[]{:S(2)}) %collective-permute-start.4) | collective-permute-done | bytes 131104 | tf_op jit(solution)/shard_map/ppermute | solution.py:20
  208.9 30.6 %while.35 = (s32[]{:T(128)}, f32[64,2048]{1,0:T(8,128)S(1)}, s32[]{:T(128)}, s32[10]{0:T(128)S(1)}, s32[10]{0:T(128)S(1)}, /*index=5*/s32[10]{0:T(128)S(1)}, bf1...) while((s32[]{:T(128)}, f32[64,2048]{1,0:T(8,128)S(1)}, ...), condition=%wide.region_26.27_spmd.clone, body=%wide.region_25.26_spmd.clone.sunk | while | flops 134349840 | bytes 3280655 | solution.py:66
  225.2 2.4 fusion.73
  235.7 2.4 fusion.73
  239.6 43.2 %all-reduce.1 = (f32[64]{0:T(128)S(1)}, f32[64]{0:T(128)S(1)}) all-reduce(f32[64]{0:T(128)S(1)} %multiply_reduce_fusion, f32[64]{0:T(128)S(1)} %get-tuple-element.263), channel_id=1, replica_groups=mesh['blk'=16,'phe'=2] {'blk'}, use_global_device_ids=true, to_apply=%region_28.29 | all-reduce | flops 128 | bytes 1024 | tf_op jit(solution)/shard_map/psum | solution.py:70
  283.5 3.1 %psum.70 = f32[]{:T(128)} all-reduce(f32[]{:T(128)} %reduce_sum.102), channel_id=1, replica_groups=mesh['blk'=16,'phe'=2] {'phe'}, use_global_device_ids=true, to_apply=%region_24.25 | all-reduce | flops 1 | bytes 8 | tf_op jit(solution)/shard_map/psum | solution.py:71
  (102 shorter events, 47.5 us)
Async XLA Ops:
  0.0 22.9 %copy-start.1 = (f32[64,1024]{1,0:T(8,128)S(1)}, f32[64,1024]{1,0:T(8,128)}, u32[]{:S(2)}) copy-start(f32[64,1024]{1,0:T(8,128)} %param.15) | copy-start | bytes 786436
  0.0 23.0 %collective-permute-start = (bf16[64,1024]{1,0:T(8,128)(2,1)S(1)}, bf16[64,1024]{1,0:T(8,128)(2,1)S(1)}, u32[]{:S(2)}, u32[]{:S(2)}) collective-permute-start(bf16[64,1024]{1,0:T(8,128)(2,1)S(1)} %convert_element_type.41), channel_id=1, source_target_pairs={{0,2},{2,4},{4,6},{6,8},{8,10},{10,12},{12,14},{14,16},{16,18},{18... | collective-permute-start | bytes 393224 | tf_op jit(solution)/shard_map/ppermute | solution.py:20
  5.0 18.0 %collective-permute-start.1 = (bf16[64,1024]{1,0:T(8,128)(2,1)S(1)}, bf16[64,1024]{1,0:T(8,128)(2,1)S(1)}, u32[]{:S(2)}, u32[]{:S(2)}) collective-permute-start(bf16[64,1024]{1,0:T(8,128)(2,1)S(1)} %convert_element_type.41), channel_id=1, source_target_pairs={{2,0},{4,2},{6,4},{8,6},{10,8},{12,10},{14,12},{16,14},{18,16},{20... | collective-permute-start | bytes 393224 | tf_op jit(solution)/shard_map/ppermute | solution.py:22
  23.1 30.7 %copy-start = (f32[64,1024]{1,0:T(8,128)S(1)}, f32[64,1024]{1,0:T(8,128)}, u32[]{:S(2)}) copy-start(f32[64,1024]{1,0:T(8,128)} %param.14) | copy-start | bytes 786436
  23.1 84.4 %copy-start.3 = (s32[64]{0:T(128)S(1)}, s32[64]{0:T(128)}, u32[]{:S(2)}) copy-start(s32[64]{0:T(128)} %param.17) | copy-start | bytes 772
  23.1 84.5 %copy-start.2 = (bf16[3,64,1024]{2,1,0:T(8,128)(2,1)S(1)}, bf16[3,64,1024]{2,1,0:T(8,128)(2,1)}, u32[]{:S(2)}) copy-start(bf16[3,64,1024]{2,1,0:T(8,128)(2,1)} %param.16) | copy-start | bytes 1179652
  107.9 9.8 %collective-permute-start.2 = (bf16[64,1024]{1,0:T(8,128)(2,1)S(1)}, bf16[64,1024]{1,0:T(8,128)(2,1)S(1)}, u32[]{:S(2)}, u32[]{:S(2)}) collective-permute-start(bf16[64,1024]{1,0:T(8,128)(2,1)S(1)} %convert_element_type.45), channel_id=1, source_target_pairs={{0,2},{2,4},{4,6},{6,8},{8,10},{10,12},{12,14},{14,16},{16,18},{18... | collective-permute-start | bytes 393224 | tf_op jit(solution)/shard_map/ppermute | solution.py:20
  111.8 7.2 %collective-permute-start.3 = (bf16[64,1024]{1,0:T(8,128)(2,1)S(1)}, bf16[64,1024]{1,0:T(8,128)(2,1)S(1)}, u32[]{:S(2)}, u32[]{:S(2)}) collective-permute-start(bf16[64,1024]{1,0:T(8,128)(2,1)S(1)} %convert_element_type.45), channel_id=1, source_target_pairs={{2,0},{4,2},{6,4},{8,6},{10,8},{12,10},{14,12},{16,14},{18,16},{20... | collective-permute-start | bytes 393224 | tf_op jit(solution)/shard_map/ppermute | solution.py:22
  197.7 9.8 %collective-permute-start.4 = (bf16[64,1024]{1,0:T(8,128)(2,1)S(1)}, bf16[64,1024]{1,0:T(8,128)(2,1)S(1)}, u32[]{:S(2)}, u32[]{:S(2)}) collective-permute-start(bf16[64,1024]{1,0:T(8,128)(2,1)S(1)} %convert_element_type.48), channel_id=1, source_target_pairs={{0,2},{2,4},{4,6},{6,8},{8,10},{10,12},{12,14},{14,16},{16,18},{18... | collective-permute-start | bytes 393224 | tf_op jit(solution)/shard_map/ppermute | solution.py:20
  201.6 7.2 %collective-permute-start.5 = (bf16[64,1024]{1,0:T(8,128)(2,1)S(1)}, bf16[64,1024]{1,0:T(8,128)(2,1)S(1)}, u32[]{:S(2)}, u32[]{:S(2)}) collective-permute-start(bf16[64,1024]{1,0:T(8,128)(2,1)S(1)} %convert_element_type.48), channel_id=1, source_target_pairs={{2,0},{4,2},{6,4},{8,6},{10,8},{12,10},{14,12},{16,14},{18,16},{20... | collective-permute-start | bytes 393224 | tf_op jit(solution)/shard_map/ppermute | solution.py:22
where the time goes:
time: 290 us; the launch traced here: 288 us
  blocking collectives  145 us (50%)
  loops' own time  40.7 us (14%)
  local copies, waits for them, and re-layouts  30 us (10%)
  matrix products  21.4 us (7%)
  other arithmetic  20.3 us (7%)
  starting transfers between devices  16.7 us (6%)
  waiting for transfers between devices  11.8 us (4%)
    psum x3, blocking collectives, shards(): resid_total = lax.psum(resid_local, 'blk')  136 us
    another operation x3, loops' own time, shards(): result = lax.fori_loop(0, seg_count, one_piece, start_value)  40.7 us
    dot_general x9, matrix products, one_piece(): lax.dot_general(window, ld_tile, (((1,), (1,)), ((), ())), preferred_elem...  21.4 us
    ppermute x3, starting transfers between devices, extended_2(): lax.ppermute(tail, axis, [(i, (i + 1) % count) for i in range(ends)])  12.9 us
    psum x3, blocking collectives, shards(): pooled_total = lax.psum(jnp.sum(scale_total), 'phe')  9.24 us
    ppermute x3, waiting for transfers between devices, extended_2(): lax.ppermute(tail, axis, [(i, (i + 1) % count) for i in range(ends)])  9.14 us
    scatter-add x1, other arithmetic, shards(): jnp.nonzero(start_mask, size=SLOTS, fill_value=snp_local)[0]  7.61 us
    dynamic_update_slice x9, local copies, waits for them, and re-layouts, one_piece(): lax.dynamic_update_slice_in_dim(result, current + product, row_start, 1)  7.52 us
  transfers between devices with their start and end apart: 6, of which 4 were waited for; matrix products, arithmetic and copies ran while one was open for 6% of the time, Pallas kernels for 0%

commit v1 on v0

--- a/solution.py
+++ b/solution.py
@@ -67,7 +67,11 @@
         applied = result[:, :snp_local]
         grad = beta_hat - applied
         resid_local = jnp.sum(grad * grad, axis=1)
-        resid_total = lax.psum(resid_local, "blk")
+        resid_total = resid_local
+        for hop in (1, 2, 4, 8):
+            resid_total = resid_total + lax.ppermute(
+                resid_total, "blk", [(dev, dev ^ hop) for dev in range(16)]
+            )
         pooled_total = lax.psum(jnp.sum(scale_total), "phe")
         pooled = pooled_total / (total_snps * total_pheno) + tiny_term
         scale = scale_total / total_snps + tiny_term

time: 290 us -> 330 us (1.14)
  starting transfers between devices: 16.7 us -> 48 us
  waiting for transfers between devices: 11.8 us -> 38.1 us
  blocking collectives: 145 us -> 127 us
    ppermute x0 -> x12, starting transfers between devices: none -> 35.6 us  [shards(): lax.ppermute(resid_total, 'blk', [(dev, dev ^ hop) for dev in range(16)])]
    ppermute x0 -> x12, waiting for transfers between devices: none -> 26.9 us  [shards(): lax.ppermute(resid_total, 'blk', [(dev, dev ^ hop) for dev in range(16)])]
    psum x3, blocking collectives: 136 us -> 118 us  [shards(): scale_total = lax.psum(scale_local, 'blk')]
    ppermute x3, waiting for transfers between devices: 9.14 us -> 4.62 us  [extended_2(): lax.ppermute(tail, axis, [(i, (i + 1) % count) for i in range(ends)])]
    ppermute x3, starting transfers between devices: 12.9 us -> 8.5 us  [extended_2(): lax.ppermute(tail, axis, [(i, (i + 1) % count) for i in range(ends)])]
    ppermute x3, waiting for transfers between devices: 2.62 us -> 6.51 us  [extended_2(): lax.ppermute(head, axis, [((i + 1) % count, i) for i in range(ends)])]
  transfers between devices with their start and end apart: 6 -> 18, of which waited for: 4 -> 12; matrix products, arithmetic and copies ran while one was open for 6% -> 6% of each run, Pallas kernels for 0% -> 0%
where the time goes in v1:
time: 330 us; the launch traced here: 328 us
  blocking collectives  127 us (38%)
  starting transfers between devices  48 us (15%)
  loops' own time  40.7 us (12%)
  waiting for transfers between devices  38.1 us (12%)
  local copies, waits for them, and re-layouts  30 us (9%)
  matrix products  21.4 us (6%)
  other arithmetic  20.3 us (6%)
    psum x3, blocking collectives, shards(): scale_total = lax.psum(scale_local, 'blk')  118 us
    another operation x3, loops' own time, shards(): result = lax.fori_loop(0, seg_count, one_piece, start_value)  40.7 us
    ppermute x12, starting transfers between devices, shards(): lax.ppermute(resid_total, 'blk', [(dev, dev ^ hop) for dev in range(16)])  35.6 us
    ppermute x12, waiting for transfers between devices, shards(): lax.ppermute(resid_total, 'blk', [(dev, dev ^ hop) for dev in range(16)])  26.9 us
    dot_general x9, matrix products, one_piece(): lax.dot_general(window, ld_tile, (((1,), (1,)), ((), ())), preferred_elem...  21.4 us
    psum x3, blocking collectives, shards(): pooled_total = lax.psum(jnp.sum(scale_total), 'phe')  9.26 us
    ppermute x3, starting transfers between devices, extended_2(): lax.ppermute(tail, axis, [(i, (i + 1) % count) for i in range(ends)])  8.5 us
    scatter-add x1, other arithmetic, shards(): jnp.nonzero(start_mask, size=SLOTS, fill_value=snp_local)[0]  7.61 us
  transfers between devices with their start and end apart: 18, of which 12 were waited for; matrix products, arithmetic and copies ran while one was open for 6% of the time, Pallas kernels for 0%

profile of v1, /device:TPU:0, one launch (start us, length us, event | category | flops | bytes accessed | tf_op | source)
XLA Modules:
  0.0 327.9 jit_solution(2444971667530388648)
XLA Ops:
  0.0 4.9 %collective-permute-start = (bf16[64,1024]{1,0:T(8,128)(2,1)S(1)}, bf16[64,1024]{1,0:T(8,128)(2,1)S(1)}, u32[]{:S(2)}, u32[]{:S(2)}) collective-permute-start(bf16[64,1024]{1,0:T(8,128)(2,1)S(1)} %convert_element_type.41), channel_id=1, source_target_pairs={{0,2},{2,4},{4,6},{6,8},{8,10},{10,12},{12,14},{14,16},{16,18},{18... | collective-permute-start | bytes 393224 | tf_op jit(solution)/shard_map/ppermute | solution.py:20
  7.5 7.6 %scatter_custom_fusion = s32[10]{0:T(128)S(1)} fusion(s32[1024]{0:T(1024)S(1)} %bitcast.48, s32[1024]{0:T(1024)S(1)} %broadcast.175, s32[]{:T(128)} %constant.110.clone.1), kind=kCustom, calls=%fused_computation.84 | custom fusion | flops 1024 | bytes 44 | tf_op jit(solution)/shard_map/scatter-add | solution.py:38
  18.6 4.0 %pad.4 = bf16[2048,1024]{1,0:T(8,128)(2,1)} pad(bf16[1024,1024]{1,0:T(8,128)(2,1)} %param.12, bf16[]{:T(256)} %constant.117.clone.1), padding=0_1024x0_0 | pad | bytes 6291458 | tf_op jit(solution)/shard_map/jit(_pad)/pad | solution.py:44
  22.9 30.7 %while.33 = (s32[]{:T(128)}, f32[64,2048]{1,0:T(8,128)S(1)}, s32[]{:T(128)}, s32[10]{0:T(128)S(1)}, s32[10]{0:T(128)S(1)}, /*index=5*/s32[10]{0:T(128)S(1)}, bf1...) while((s32[]{:T(128)}, f32[64,2048]{1,0:T(8,128)S(1)}, ...), condition=%wide.region_10.11_spmd.clone, body=%wide.region_9.10_spmd.clone.sunk | while | flops 134349840 | bytes 3280655 | solution.py:66
  53.9 3.4 %collective-permute-done.2 = f32[64]{0:T(128)S(1)} collective-permute-done((f32[64]{0:T(128)S(1)}, f32[64]{0:T(128)S(1)}, u32[]{:S(2)}, u32[]{:S(2)}) %collective-permute-start.2) | collective-permute-done | bytes 288 | tf_op jit(solution)/shard_map/ppermute | solution.py:72
  57.3 13.3 %collective-permute-start.3 = (f32[64]{0:T(128)S(1)}, f32[64]{0:T(128)S(1)}, u32[]{:S(2)}, u32[]{:S(2)}) collective-permute-start(f32[64]{0:T(128)S(1)} %add.256), channel_id=1, source_target_pairs={{0,4},{2,6},{4,0},{6,2},{8,12},{10,14},{12,8},{14,10},{16,20},{18,... | collective-permute-start | bytes 776 | tf_op jit(solution)/shard_map/ppermute | solution.py:72
  70.6 39.6 %psum.42 = f32[64]{0:T(128)S(1)} all-reduce(f32[64]{0:T(128)S(1)} %divide_reduce_fusion), channel_id=1, replica_groups=mesh['blk'=16,'phe'=2] {'blk'}, use_global_device_ids=true, to_apply=%region_1.2 | all-reduce | flops 64 | bytes 512 | tf_op jit(solution)/shard_map/psum | solution.py:51
  110.8 3.1 psum.43
  114.6 4.4 %collective-permute-done.5 = f32[64]{0:T(128)S(1)} collective-permute-done((f32[64]{0:T(128)S(1)}, f32[64]{0:T(128)S(1)}, u32[]{:S(2)}, u32[]{:S(2)}) %collective-permute-start.5) | collective-permute-done | bytes 288 | tf_op jit(solution)/shard_map/ppermute | solution.py:72
  123.2 4.4 %collective-permute-done.7 = bf16[64,1024]{1,0:T(8,128)(2,1)S(1)} collective-permute-done((bf16[64,1024]{1,0:T(8,128)(2,1)S(1)}, bf16[64,1024]{1,0:T(8,128)(2,1)S(1)}, u32[]{:S(2)}, u32[]{:S(2)}) %collective-permute-start.7) | collective-permute-done | bytes 131104 | tf_op jit(solution)/shard_map/ppermute | solution.py:22
  127.7 30.6 %while.34 = (s32[]{:T(128)}, f32[64,2048]{1,0:T(8,128)S(1)}, s32[]{:T(128)}, s32[10]{0:T(128)S(1)}, s32[10]{0:T(128)S(1)}, /*index=5*/s32[10]{0:T(128)S(1)}, bf1...) while((s32[]{:T(128)}, f32[64,2048]{1,0:T(8,128)S(1)}, ...), condition=%wide.region_17.18_spmd.clone, body=%wide.region_16.17_spmd.clone.sunk | while | flops 134349840 | bytes 3280655 | solution.py:66
  158.5 3.6 %collective-permute-done.8 = f32[64]{0:T(128)S(1)} collective-permute-done((f32[64]{0:T(128)S(1)}, f32[64]{0:T(128)S(1)}, u32[]{:S(2)}, u32[]{:S(2)}) %collective-permute-start.8) | collective-permute-done | bytes 288 | tf_op jit(solution)/shard_map/ppermute | solution.py:72
  162.0 13.2 %collective-permute-start.9 = (f32[64]{0:T(128)S(1)}, f32[64]{0:T(128)S(1)}, u32[]{:S(2)}, u32[]{:S(2)}) collective-permute-start(f32[64]{0:T(128)S(1)} %add.269), channel_id=1, source_target_pairs={{0,4},{2,6},{4,0},{6,2},{8,12},{10,14},{12,8},{14,10},{16,20},{18,... | collective-permute-start | bytes 776 | tf_op jit(solution)/shard_map/ppermute | solution.py:72
  176.8 38.2 %psum.44 = f32[64]{0:T(128)S(1)} all-reduce(f32[64]{0:T(128)S(1)} %get-tuple-element.259), channel_id=1, replica_groups=mesh['blk'=16,'phe'=2] {'blk'}, use_global_device_ids=true, to_apply=%region_13.14 | all-reduce | flops 64 | bytes 512 | tf_op jit(solution)/shard_map/psum | solution.py:51
  215.6 3.1 psum.45
  219.4 4.4 %collective-permute-done.11 = f32[64]{0:T(128)S(1)} collective-permute-done((f32[64]{0:T(128)S(1)}, f32[64]{0:T(128)S(1)}, u32[]{:S(2)}, u32[]{:S(2)}) %collective-permute-start.11) | collective-permute-done | bytes 288 | tf_op jit(solution)/shard_map/ppermute | solution.py:72
  227.8 3.4 %collective-permute-done.12 = bf16[64,1024]{1,0:T(8,128)(2,1)S(1)} collective-permute-done((bf16[64,1024]{1,0:T(8,128)(2,1)S(1)}, bf16[64,1024]{1,0:T(8,128)(2,1)S(1)}, u32[]{:S(2)}, u32[]{:S(2)}) %collective-permute-start.12) | collective-permute-done | bytes 131104 | tf_op jit(solution)/shard_map/ppermute | solution.py:20
  233.4 30.6 %while.35 = (s32[]{:T(128)}, f32[64,2048]{1,0:T(8,128)S(1)}, s32[]{:T(128)}, s32[10]{0:T(128)S(1)}, s32[10]{0:T(128)S(1)}, /*index=5*/s32[10]{0:T(128)S(1)}, bf1...) while((s32[]{:T(128)}, f32[64,2048]{1,0:T(8,128)S(1)}, ...), condition=%wide.region_24.25_spmd.clone, body=%wide.region_23.24_spmd.clone.sunk | while | flops 134349840 | bytes 3280655 | solution.py:66
  249.7 2.4 fusion.73
  264.2 3.6 %collective-permute-done.14 = f32[64]{0:T(128)S(1)} collective-permute-done((f32[64]{0:T(128)S(1)}, f32[64]{0:T(128)S(1)}, u32[]{:S(2)}, u32[]{:S(2)}) %collective-permute-start.14) | collective-permute-done | bytes 288 | tf_op jit(solution)/shard_map/ppermute | solution.py:72
  267.8 8.7 %collective-permute-start.15 = (f32[64]{0:T(128)S(1)}, f32[64]{0:T(128)S(1)}, u32[]{:S(2)}, u32[]{:S(2)}) collective-permute-start(f32[64]{0:T(128)S(1)} %add.282), channel_id=1, source_target_pairs={{0,4},{2,6},{4,0},{6,2},{8,12},{10,14},{12,8},{14,10},{16,20},{18,... | collective-permute-start | bytes 776 | tf_op jit(solution)/shard_map/ppermute | solution.py:72
  278.1 40.1 %psum.46 = f32[64]{0:T(128)S(1)} all-reduce(f32[64]{0:T(128)S(1)} %get-tuple-element.257), channel_id=1, replica_groups=mesh['blk'=16,'phe'=2] {'blk'}, use_global_device_ids=true, to_apply=%region_20.21 | all-reduce | flops 64 | bytes 512 | tf_op jit(solution)/shard_map/psum | solution.py:51
  318.8 3.1 psum.47
  322.6 4.4 %collective-permute-done.17 = f32[64]{0:T(128)S(1)} collective-permute-done((f32[64]{0:T(128)S(1)}, f32[64]{0:T(128)S(1)}, u32[]{:S(2)}, u32[]{:S(2)}) %collective-permute-start.17) | collective-permute-done | bytes 288 | tf_op jit(solution)/shard_map/ppermute | solution.py:72
  (135 shorter events, 72.1 us)
Async XLA Ops:
  0.0 22.7 %collective-permute-start = (bf16[64,1024]{1,0:T(8,128)(2,1)S(1)}, bf16[64,1024]{1,0:T(8,128)(2,1)S(1)}, u32[]{:S(2)}, u32[]{:S(2)}) collective-permute-start(bf16[64,1024]{1,0:T(8,128)(2,1)S(1)} %convert_element_type.41), channel_id=1, source_target_pairs={{0,2},{2,4},{4,6},{6,8},{8,10},{10,12},{12,14},{14,16},{16,18},{18... | collective-permute-start | bytes 393224 | tf_op jit(solution)/shard_map/ppermute | solution.py:20
  4.9 17.8 %collective-permute-start.1 = (bf16[64,1024]{1,0:T(8,128)(2,1)S(1)}, bf16[64,1024]{1,0:T(8,128)(2,1)S(1)}, u32[]{:S(2)}, u32[]{:S(2)}) collective-permute-start(bf16[64,1024]{1,0:T(8,128)(2,1)S(1)} %convert_element_type.41), channel_id=1, source_target_pairs={{2,0},{4,2},{6,4},{8,6},{10,8},{12,10},{14,12},{16,14},{18,16},{20... | collective-permute-start | bytes 393224 | tf_op jit(solution)/shard_map/ppermute | solution.py:22
  22.8 30.7 %copy-start = (f32[64,1024]{1,0:T(8,128)S(1)}, f32[64,1024]{1,0:T(8,128)}, u32[]{:S(2)}) copy-start(f32[64,1024]{1,0:T(8,128)} %param.14) | copy-start | bytes 786436
  22.8 30.9 %copy-start.1 = (f32[64,1024]{1,0:T(8,128)S(1)}, f32[64,1024]{1,0:T(8,128)}, u32[]{:S(2)}) copy-start(f32[64,1024]{1,0:T(8,128)} %param.15) | copy-start | bytes 786436
  22.8 96.3 %copy-start.3 = (s32[64]{0:T(128)S(1)}, s32[64]{0:T(128)}, u32[]{:S(2)}) copy-start(s32[64]{0:T(128)} %param.17) | copy-start | bytes 772
  22.8 96.3 %copy-start.2 = (bf16[3,64,1024]{2,1,0:T(8,128)(2,1)S(1)}, bf16[3,64,1024]{2,1,0:T(8,128)(2,1)}, u32[]{:S(2)}) copy-start(bf16[3,64,1024]{2,1,0:T(8,128)(2,1)} %param.16) | copy-start | bytes 1179652
  53.7 3.6 %collective-permute-start.2 = (f32[64]{0:T(128)S(1)}, f32[64]{0:T(128)S(1)}, u32[]{:S(2)}, u32[]{:S(2)}) collective-permute-start(f32[64]{0:T(128)S(1)} %multiply_reduce_fusion.2), channel_id=1, source_target_pairs={{0,2},{2,0},{4,6},{6,4},{8,10},{10,8},{12,14},{14,12},{16,18},{18,... | collective-permute-start | bytes 776 | tf_op jit(solution)/shard_map/ppermute | solution.py:72
  57.3 53.5 %collective-permute-start.3 = (f32[64]{0:T(128)S(1)}, f32[64]{0:T(128)S(1)}, u32[]{:S(2)}, u32[]{:S(2)}) collective-permute-start(f32[64]{0:T(128)S(1)} %add.256), channel_id=1, source_target_pairs={{0,4},{2,6},{4,0},{6,2},{8,12},{10,14},{12,8},{14,10},{16,20},{18,... | collective-permute-start | bytes 776 | tf_op jit(solution)/shard_map/ppermute | solution.py:72
  110.8 3.8 %collective-permute-start.4 = (f32[64]{0:T(128)S(1)}, f32[64]{0:T(128)S(1)}, u32[]{:S(2)}, u32[]{:S(2)}) collective-permute-start(f32[64]{0:T(128)S(1)} %add.257), channel_id=1, source_target_pairs={{0,8},{2,10},{4,12},{6,14},{8,0},{10,2},{12,4},{14,6},{16,24},{18,... | collective-permute-start | bytes 776 | tf_op jit(solution)/shard_map/ppermute | solution.py:72
  114.6 4.5 %collective-permute-start.5 = (f32[64]{0:T(128)S(1)}, f32[64]{0:T(128)S(1)}, u32[]{:S(2)}, u32[]{:S(2)}) collective-permute-start(f32[64]{0:T(128)S(1)} %add.258), channel_id=1, source_target_pairs={{0,16},{2,18},{4,20},{6,22},{8,24},{10,26},{12,28},{14,30},{16,0},... | collective-permute-start | bytes 776 | tf_op jit(solution)/shard_map/ppermute | solution.py:72
  119.4 3.8 %collective-permute-start.6 = (bf16[64,1024]{1,0:T(8,128)(2,1)S(1)}, bf16[64,1024]{1,0:T(8,128)(2,1)S(1)}, u32[]{:S(2)}, u32[]{:S(2)}) collective-permute-start(bf16[64,1024]{1,0:T(8,128)(2,1)S(1)} %convert_element_type.45), channel_id=1, source_target_pairs={{0,2},{2,4},{4,6},{6,8},{8,10},{10,12},{12,14},{14,16},{16,18},{18... | collective-permute-start | bytes 393224 | tf_op jit(solution)/shard_map/ppermute | solution.py:20
  120.7 6.9 %collective-permute-start.7 = (bf16[64,1024]{1,0:T(8,128)(2,1)S(1)}, bf16[64,1024]{1,0:T(8,128)(2,1)S(1)}, u32[]{:S(2)}, u32[]{:S(2)}) collective-permute-start(bf16[64,1024]{1,0:T(8,128)(2,1)S(1)} %convert_element_type.45), channel_id=1, source_target_pairs={{2,0},{4,2},{6,4},{8,6},{10,8},{12,10},{14,12},{16,14},{18,16},{20... | collective-permute-start | bytes 393224 | tf_op jit(solution)/shard_map/ppermute | solution.py:22
  158.4 3.6 %collective-permute-start.8 = (f32[64]{0:T(128)S(1)}, f32[64]{0:T(128)S(1)}, u32[]{:S(2)}, u32[]{:S(2)}) collective-permute-start(f32[64]{0:T(128)S(1)} %multiply_reduce_fusion.1), channel_id=1, source_target_pairs={{0,2},{2,0},{4,6},{6,4},{8,10},{10,8},{12,14},{14,12},{16,18},{18,... | collective-permute-start | bytes 776 | tf_op jit(solution)/shard_map/ppermute | solution.py:72
  162.0 14.8 %collective-permute-start.9 = (f32[64]{0:T(128)S(1)}, f32[64]{0:T(128)S(1)}, u32[]{:S(2)}, u32[]{:S(2)}) collective-permute-start(f32[64]{0:T(128)S(1)} %add.269), channel_id=1, source_target_pairs={{0,4},{2,6},{4,0},{6,2},{8,12},{10,14},{12,8},{14,10},{16,20},{18,... | collective-permute-start | bytes 776 | tf_op jit(solution)/shard_map/ppermute | solution.py:72
  176.8 42.5 %collective-permute-start.10 = (f32[64]{0:T(128)S(1)}, f32[64]{0:T(128)S(1)}, u32[]{:S(2)}, u32[]{:S(2)}) collective-permute-start(f32[64]{0:T(128)S(1)} %add.270), channel_id=1, source_target_pairs={{0,8},{2,10},{4,12},{6,14},{8,0},{10,2},{12,4},{14,6},{16,24},{18,... | collective-permute-start | bytes 776 | tf_op jit(solution)/shard_map/ppermute | solution.py:72
  219.3 4.5 %collective-permute-start.11 = (f32[64]{0:T(128)S(1)}, f32[64]{0:T(128)S(1)}, u32[]{:S(2)}, u32[]{:S(2)}) collective-permute-start(f32[64]{0:T(128)S(1)} %add.271), channel_id=1, source_target_pairs={{0,16},{2,18},{4,20},{6,22},{8,24},{10,26},{12,28},{14,30},{16,0},... | collective-permute-start | bytes 776 | tf_op jit(solution)/shard_map/ppermute | solution.py:72
  224.2 7.1 %collective-permute-start.12 = (bf16[64,1024]{1,0:T(8,128)(2,1)S(1)}, bf16[64,1024]{1,0:T(8,128)(2,1)S(1)}, u32[]{:S(2)}, u32[]{:S(2)}) collective-permute-start(bf16[64,1024]{1,0:T(8,128)(2,1)S(1)} %convert_element_type.48), channel_id=1, source_target_pairs={{0,2},{2,4},{4,6},{6,8},{8,10},{10,12},{12,14},{14,16},{16,18},{18... | collective-permute-start | bytes 393224 | tf_op jit(solution)/shard_map/ppermute | solution.py:20
  226.5 6.9 %collective-permute-start.13 = (bf16[64,1024]{1,0:T(8,128)(2,1)S(1)}, bf16[64,1024]{1,0:T(8,128)(2,1)S(1)}, u32[]{:S(2)}, u32[]{:S(2)}) collective-permute-start(bf16[64,1024]{1,0:T(8,128)(2,1)S(1)} %convert_element_type.48), channel_id=1, source_target_pairs={{2,0},{4,2},{6,4},{8,6},{10,8},{12,10},{14,12},{16,14},{18,16},{20... | collective-permute-start | bytes 393224 | tf_op jit(solution)/shard_map/ppermute | solution.py:22
  264.2 3.6 %collective-permute-start.14 = (f32[64]{0:T(128)S(1)}, f32[64]{0:T(128)S(1)}, u32[]{:S(2)}, u32[]{:S(2)}) collective-permute-start(f32[64]{0:T(128)S(1)} %multiply_reduce_fusion), channel_id=1, source_target_pairs={{0,2},{2,0},{4,6},{6,4},{8,10},{10,8},{12,14},{14,12},{16,18},{18,... | collective-permute-start | bytes 776 | tf_op jit(solution)/shard_map/ppermute | solution.py:72
  267.8 10.3 %collective-permute-start.15 = (f32[64]{0:T(128)S(1)}, f32[64]{0:T(128)S(1)}, u32[]{:S(2)}, u32[]{:S(2)}) collective-permute-start(f32[64]{0:T(128)S(1)} %add.282), channel_id=1, source_target_pairs={{0,4},{2,6},{4,0},{6,2},{8,12},{10,14},{12,8},{14,10},{16,20},{18,... | collective-permute-start | bytes 776 | tf_op jit(solution)/shard_map/ppermute | solution.py:72
  278.1 44.5 %collective-permute-start.16 = (f32[64]{0:T(128)S(1)}, f32[64]{0:T(128)S(1)}, u32[]{:S(2)}, u32[]{:S(2)}) collective-permute-start(f32[64]{0:T(128)S(1)} %add.283), channel_id=1, source_target_pairs={{0,8},{2,10},{4,12},{6,14},{8,0},{10,2},{12,4},{14,6},{16,24},{18,... | collective-permute-start | bytes 776 | tf_op jit(solution)/shard_map/ppermute | solution.py:72
  322.5 4.5 %collective-permute-start.17 = (f32[64]{0:T(128)S(1)}, f32[64]{0:T(128)S(1)}, u32[]{:S(2)}, u32[]{:S(2)}) collective-permute-start(f32[64]{0:T(128)S(1)} %add.284), channel_id=1, source_target_pairs={{0,16},{2,18},{4,20},{6,22},{8,24},{10,26},{12,28},{14,30},{16,0},... | collective-permute-start | bytes 776 | tf_op jit(solution)/shard_map/ppermute | solution.py:72
